TPU v7x, 32 devices: a whole 2x2x4 slice. The times are simulated.
32 devices in a mesh: slab: 2 (over core), py: 4 (over z), pz: 4 (over y, x).
Axes of the slice: x: 2, y: 2, z: 4, core: 2. Of those that a mesh axis runs over, the one named last changes fastest.
Arguments:
- start_vector: float32 [32, 128, 256], P('pz', 'py', 'slab'), may hold values from -6 to 6
- potential: float32 [32, 128, 256], P('pz', 'py', 'slab'), may hold values from 0.5 to 4
Outputs:
- krylov_basis: float32 [6, 32, 128, 256], P(None, 'pz', 'py', 'slab')
- tridiagonal: float32 [2, 5], replicated
All inputs are finite; a program needn't handle non-finite values.
Results may differ from a plain program's by a relative error of at most 0.00012.
Values sent between devices are 32-bit elements; how exact they have to be, the bound alone decides.
A program may use at most 64 MiB of HBM per device.

v0:
```python
import jax
import jax.numpy as jnp
from jax import lax
from jax.sharding import PartitionSpec as P

ITERS = 5


EPSILON = 1e-06


def with_halo(block, sides, width):
    for axis, dim in sides:
        count = lax.axis_size(axis)
        forward = [(i, i + 1) for i in range(count - 1)]
        backward = [(target, source) for source, target in forward]
        low = lax.ppermute(
            lax.slice_in_dim(block, block.shape[dim] - width, None, axis=dim), axis, forward
        )
        high = lax.ppermute(lax.slice_in_dim(block, 0, width, axis=dim), axis, backward)
        block = jnp.concatenate([low, block, high], axis=dim)
    return block


def apply_hamiltonian(field, potential):
    padded = with_halo(field, (("slab", 2), ("py", 1), ("pz", 0)), 1)
    beside = padded[2:, 1:-1, 1:-1] + padded[:-2, 1:-1, 1:-1]
    beside = beside + padded[1:-1, 2:, 1:-1] + padded[1:-1, :-2, 1:-1]
    beside = beside + padded[1:-1, 1:-1, 2:] + padded[1:-1, 1:-1, :-2]
    return (6.0 + potential) * field - beside


def reduce_all(partials):
    inner = lax.psum(partials, "pz")
    return lax.psum(inner, ("slab", "py"))


def project(active, image):
    return jnp.einsum("kzyx,zyx->k", active, image, precision=lax.Precision.HIGHEST)


def remove(image, coeffs, active):
    return image - jnp.einsum("k,kzyx->zyx", coeffs, active, precision=lax.Precision.HIGHEST)


def shards(start_vector, potential):
    cell_count = (
        start_vector.size * lax.axis_size("slab") * lax.axis_size("py") * lax.axis_size("pz")
    )
    per_cell = jnp.float32(1.0 / cell_count)
    start_norm = reduce_all(jnp.sum(start_vector * start_vector).reshape(1))[0] * per_cell
    vectors = [start_vector / jnp.sqrt(start_norm + EPSILON)]
    alphas = []
    beta_list = []
    for iteration in range(ITERS):
        image = apply_hamiltonian(vectors[-1], potential)
        active = jnp.stack(vectors)
        first_coeff = reduce_all(project(active, image)) * per_cell
        image = remove(image, first_coeff, active)
        local_second = project(active, image)
        summed = (
            reduce_all(jnp.concatenate([local_second, jnp.sum(image * image).reshape(1)]))
            * per_cell
        )
        second_coeff = summed[:-1]
        image = remove(image, second_coeff, active)
        square_mean = summed[-1] - jnp.sum(second_coeff * second_coeff)
        beta_value = jnp.sqrt(square_mean + EPSILON)
        alphas.append(first_coeff[iteration] + second_coeff[iteration])
        beta_list.append(beta_value)
        vectors.append(image / beta_value)
    return (jnp.stack(vectors), jnp.stack([jnp.stack(alphas), jnp.stack(beta_list)]))


def solution(mesh):
    in_specs = (P("pz", "py", "slab"), P("pz", "py", "slab"))
    out_specs = (P(None, "pz", "py", "slab"), P())
    return jax.shard_map(shards, mesh=mesh, in_specs=in_specs, out_specs=out_specs, check_vma=False)
```

profile of v0, /device:TPU:0, one launch (start us, length us, event | category | flops | bytes accessed | tf_op | source)
XLA Modules:
  0.0 438.7 jit_solution(16922644488798986109)
XLA Ops:
  2.2 12.0 %psum.154 = f32[1]{0:T(128)} all-reduce(f32[1]{0:T(128)} %bitcast.4), channel_id=1, replica_groups=mesh['slab'=2,'py'=4,'pz'=4] {'pz'}, use_global_device_ids=true, to_apply=%region_1.0 | all-reduce | flops 1 | bytes 8 | tf_op jit(solution)/shard_map/psum | solution.py:34
  14.2 16.0 %psum.155 = f32[1]{0:T(128)} all-reduce(f32[1]{0:T(128)} %psum.154), channel_id=1, replica_groups=mesh['slab'=2,'py'=4,'pz'=4] {'slab','py'}, use_global_device_ids=true, to_apply=%region_2.0 | all-reduce | flops 1 | bytes 8 | tf_op jit(solution)/shard_map/psum | solution.py:35
  31.1 3.9 collective-permute-start
  41.1 4.2 collective-permute-done.3
  48.7 4.6 %collective-permute-done.4 = f32[1,34,130]{2,1,0:T(8,128)S(1)} collective-permute-done((f32[1,34,130]{2,1,0:T(8,128)S(1)}, f32[1,34,130]{2,1,0:T(8,128)S(1)}, u32[]{:S(2)}, u32[]{:S(2)}) %collective-permute-start.4) | collective-permute-done | bytes 17712 | tf_op jit(solution)/shard_map/ppermute | solution.py:20
  54.2 11.0 %psum.156 = f32[1]{0:T(128)} all-reduce(f32[1]{0:T(128)} %bitcast.7), channel_id=1, replica_groups=mesh['slab'=2,'py'=4,'pz'=4] {'pz'}, use_global_device_ids=true, to_apply=%region_3.0 | all-reduce | flops 1 | bytes 8 | tf_op jit(solution)/shard_map/psum | solution.py:34
  65.2 14.7 %psum.157 = f32[1]{0:T(128)} all-reduce(f32[1]{0:T(128)} %psum.156), channel_id=1, replica_groups=mesh['slab'=2,'py'=4,'pz'=4] {'slab','py'}, use_global_device_ids=true, to_apply=%region_4.0 | all-reduce | flops 1 | bytes 8 | tf_op jit(solution)/shard_map/psum | solution.py:35
  83.3 7.4 %psum.158 = f32[2]{0:T(128)S(1)} all-reduce(f32[2]{0:T(128)S(1)} %pad_maximum_fusion.134), channel_id=1, replica_groups=mesh['slab'=2,'py'=4,'pz'=4] {'pz'}, use_global_device_ids=true, to_apply=%region_6.0 | all-reduce | flops 2 | bytes 16 | tf_op jit(solution)/shard_map/psum | solution.py:34
  90.7 15.6 %psum.159 = f32[2]{0:T(128)S(1)} all-reduce(f32[2]{0:T(128)S(1)} %psum.158), channel_id=1, replica_groups=mesh['slab'=2,'py'=4,'pz'=4] {'slab','py'}, use_global_device_ids=true, to_apply=%region_7.0 | all-reduce | flops 2 | bytes 16 | tf_op jit(solution)/shard_map/psum | solution.py:35
  109.8 2.0 collective-permute-start.6
  118.1 4.2 collective-permute-done.9
  122.4 3.9 collective-permute-start.11
  128.0 4.2 collective-permute-done.10
  132.5 2.4 convolution_bitcast_fusion.5
  135.0 9.3 %psum.160 = f32[2]{0:T(128)S(1)} all-reduce(f32[2]{0:T(128)S(1)} %convolution_bitcast_fusion.5), channel_id=1, replica_groups=mesh['slab'=2,'py'=4,'pz'=4] {'pz'}, use_global_device_ids=true, to_apply=%region_8.0 | all-reduce | flops 2 | bytes 16 | tf_op jit(solution)/shard_map/psum | solution.py:34
  144.2 14.4 %psum.161 = f32[2]{0:T(128)S(1)} all-reduce(f32[2]{0:T(128)S(1)} %psum.160), channel_id=1, replica_groups=mesh['slab'=2,'py'=4,'pz'=4] {'slab','py'}, use_global_device_ids=true, to_apply=%region_9.0 | all-reduce | flops 2 | bytes 16 | tf_op jit(solution)/shard_map/psum | solution.py:35
  160.3 2.4 convolution_bitcast_fusion.4
  163.3 8.5 %psum.162 = f32[3]{0:T(128)S(1)} all-reduce(f32[3]{0:T(128)S(1)} %pad_maximum_fusion.135), channel_id=1, replica_groups=mesh['slab'=2,'py'=4,'pz'=4] {'pz'}, use_global_device_ids=true, to_apply=%region_11.0 | all-reduce | flops 3 | bytes 24 | tf_op jit(solution)/shard_map/psum | solution.py:34
  171.8 15.2 %psum.163 = f32[3]{0:T(128)S(1)} all-reduce(f32[3]{0:T(128)S(1)} %psum.162), channel_id=1, replica_groups=mesh['slab'=2,'py'=4,'pz'=4] {'slab','py'}, use_global_device_ids=true, to_apply=%region_12.0 | all-reduce | flops 3 | bytes 24 | tf_op jit(solution)/shard_map/psum | solution.py:35
  190.7 2.0 collective-permute-start.12
  199.4 4.2 collective-permute-done.15
  203.7 2.9 collective-permute-start.17
  208.2 4.2 collective-permute-done.16
  212.8 2.4 convolution_bitcast_fusion.3
  215.2 9.4 %psum.164 = f32[3]{0:T(128)S(1)} all-reduce(f32[3]{0:T(128)S(1)} %convolution_bitcast_fusion.3), channel_id=1, replica_groups=mesh['slab'=2,'py'=4,'pz'=4] {'pz'}, use_global_device_ids=true, to_apply=%region_14.0 | all-reduce | flops 3 | bytes 24 | tf_op jit(solution)/shard_map/psum | solution.py:34
  224.6 14.2 %psum.165 = f32[3]{0:T(128)S(1)} all-reduce(f32[3]{0:T(128)S(1)} %psum.164), channel_id=1, replica_groups=mesh['slab'=2,'py'=4,'pz'=4] {'slab','py'}, use_global_device_ids=true, to_apply=%region_15.0 | all-reduce | flops 3 | bytes 24 | tf_op jit(solution)/shard_map/psum | solution.py:35
  240.7 2.4 convolution_bitcast_fusion.2
  243.8 8.3 %psum.166 = f32[4]{0:T(128)S(1)} all-reduce(f32[4]{0:T(128)S(1)} %pad_maximum_fusion.136), channel_id=1, replica_groups=mesh['slab'=2,'py'=4,'pz'=4] {'pz'}, use_global_device_ids=true, to_apply=%region_17.0 | all-reduce | flops 4 | bytes 32 | tf_op jit(solution)/shard_map/psum | solution.py:34
  252.1 15.6 %psum.167 = f32[4]{0:T(128)S(1)} all-reduce(f32[4]{0:T(128)S(1)} %psum.166), channel_id=1, replica_groups=mesh['slab'=2,'py'=4,'pz'=4] {'slab','py'}, use_global_device_ids=true, to_apply=%region_18.0 | all-reduce | flops 4 | bytes 32 | tf_op jit(solution)/shard_map/psum | solution.py:35
  271.5 2.0 collective-permute-start.18
  279.8 4.2 collective-permute-done.21
  284.1 3.1 collective-permute-start.23
  288.8 4.2 collective-permute-done.22
  293.4 2.6 convolution_bitcast_fusion.1
  295.9 9.3 %psum.168 = f32[4]{0:T(128)S(1)} all-reduce(f32[4]{0:T(128)S(1)} %convolution_bitcast_fusion.1), channel_id=1, replica_groups=mesh['slab'=2,'py'=4,'pz'=4] {'pz'}, use_global_device_ids=true, to_apply=%region_20.0 | all-reduce | flops 4 | bytes 32 | tf_op jit(solution)/shard_map/psum | solution.py:34
  305.2 14.4 %psum.169 = f32[4]{0:T(128)S(1)} all-reduce(f32[4]{0:T(128)S(1)} %psum.168), channel_id=1, replica_groups=mesh['slab'=2,'py'=4,'pz'=4] {'slab','py'}, use_global_device_ids=true, to_apply=%region_21.0 | all-reduce | flops 4 | bytes 32 | tf_op jit(solution)/shard_map/psum | solution.py:35
  321.5 2.6 convolution_bitcast_fusion
  325.4 8.5 %psum.170 = f32[5]{0:T(128)S(1)} all-reduce(f32[5]{0:T(128)S(1)} %pad_maximum_fusion.137), channel_id=1, replica_groups=mesh['slab'=2,'py'=4,'pz'=4] {'pz'}, use_global_device_ids=true, to_apply=%region_23.0 | all-reduce | flops 5 | bytes 40 | tf_op jit(solution)/shard_map/psum | solution.py:34
  333.9 15.2 %psum.171 = f32[5]{0:T(128)S(1)} all-reduce(f32[5]{0:T(128)S(1)} %psum.170), channel_id=1, replica_groups=mesh['slab'=2,'py'=4,'pz'=4] {'slab','py'}, use_global_device_ids=true, to_apply=%region_24.0 | all-reduce | flops 5 | bytes 40 | tf_op jit(solution)/shard_map/psum | solution.py:35
  361.8 4.0 collective-permute-done.27
  365.9 2.9 collective-permute-start.29
  372.0 2.7 collective-permute-done.28
  375.1 2.5 fusion.8
  377.6 9.4 %psum.172 = f32[5]{0:T(128)S(1)} all-reduce(f32[5]{0:T(128)S(1)} %fusion.8), channel_id=1, replica_groups=mesh['slab'=2,'py'=4,'pz'=4] {'pz'}, use_global_device_ids=true, to_apply=%region_26.0 | all-reduce | flops 5 | bytes 40 | tf_op jit(solution)/shard_map/psum | solution.py:34
  387.0 14.0 %psum.173 = f32[5]{0:T(128)S(1)} all-reduce(f32[5]{0:T(128)S(1)} %psum.172), channel_id=1, replica_groups=mesh['slab'=2,'py'=4,'pz'=4] {'slab','py'}, use_global_device_ids=true, to_apply=%region_27.0 | all-reduce | flops 5 | bytes 40 | tf_op jit(solution)/shard_map/psum | solution.py:35
  403.0 2.5 fusion.11
  406.8 8.3 %psum.174 = f32[6]{0:T(128)S(1)} all-reduce(f32[6]{0:T(128)S(1)} %pad_maximum_fusion.138), channel_id=1, replica_groups=mesh['slab'=2,'py'=4,'pz'=4] {'pz'}, use_global_device_ids=true, to_apply=%region_29.0 | all-reduce | flops 6 | bytes 48 | tf_op jit(solution)/shard_map/psum | solution.py:34
  416.4 15.6 %psum.175 = f32[6]{0:T(128)S(1)} all-reduce(f32[6]{0:T(128)S(1)} %psum.174), channel_id=1, replica_groups=mesh['slab'=2,'py'=4,'pz'=4] {'slab','py'}, use_global_device_ids=true, to_apply=%region_30.0 | all-reduce | flops 6 | bytes 48 | tf_op jit(solution)/shard_map/psum | solution.py:35
  (126 shorter events, 73.6 us)
Async XLA Ops:
  0.6 30.3 %copy-start.1 = (f32[8,32,128]{2,1,0:T(8,128)S(1)}, f32[8,32,128]{2,1,0:T(8,128)}, u32[]{:S(2)}) copy-start(f32[8,32,128]{2,1,0:T(8,128)} %param.2) | copy-start | bytes 393220
  31.1 5.2 %collective-permute-start = (f32[8,32,1]{2,1,0:T(8,128)S(1)}, f32[8,32,1]{2,1,0:T(8,128)S(1)}, u32[]{:S(2)}, u32[]{:S(2)}) collective-permute-start(f32[8,32,1]{2,1,0:T(8,128)S(1)} %get-tuple-element.52), channel_id=1, source_target_pairs={{0,16},{1,17},{2,18},{3,19},{4,20},{5,21},{6,22},{7,23},{8,24},{9,... | collective-permute-start | bytes 3080 | tf_op jit(solution)/shard_map/ppermute | solution.py:17
  35.0 3.2 collective-permute-start.1
  38.4 2.7 collective-permute-start.2
  39.7 13.6 %copy-start = (f32[8,32,128]{2,1,0:T(8,128)S(1)}, f32[8,32,128]{2,1,0:T(8,128)}, u32[]{:S(2)}) copy-start(f32[8,32,128]{2,1,0:T(8,128)} %param.3) | copy-start | bytes 393220
  39.7 5.7 %collective-permute-start.3 = (f32[8,1,130]{2,1,0:T(1,128)S(1)}, f32[8,1,130]{2,1,0:T(1,128)S(1)}, u32[]{:S(2)}, u32[]{:S(2)}) collective-permute-start(f32[8,1,130]{2,1,0:T(1,128)S(1)} %get-tuple-element.40), channel_id=1, source_target_pairs={{4,0},{8,4},{12,8},{5,1},{9,5},{13,9},{6,2},{10,6},{14,10},{7,3},{... | collective-permute-start | bytes 12488 | tf_op jit(solution)/shard_map/ppermute | solution.py:20
  45.5 3.2 collective-permute-start.5
  47.0 6.3 %collective-permute-start.4 = (f32[1,34,130]{2,1,0:T(8,128)S(1)}, f32[1,34,130]{2,1,0:T(8,128)S(1)}, u32[]{:S(2)}, u32[]{:S(2)}) collective-permute-start(f32[1,34,130]{2,1,0:T(8,128)S(1)} %get-tuple-element.30), channel_id=1, source_target_pairs={{1,0},{2,1},{3,2},{5,4},{6,5},{7,6},{9,8},{10,9},{11,10},{13,12},{... | collective-permute-start | bytes 53048 | tf_op jit(solution)/shard_map/ppermute | solution.py:20
  109.8 3.3 collective-permute-start.6
  111.8 3.2 collective-permute-start.7
  115.2 2.9 collective-permute-start.8
  116.7 5.5 %collective-permute-start.9 = (f32[8,1,130]{2,1,0:T(1,128)S(1)}, f32[8,1,130]{2,1,0:T(1,128)S(1)}, u32[]{:S(2)}, u32[]{:S(2)}) collective-permute-start(f32[8,1,130]{2,1,0:T(1,128)S(1)} %get-tuple-element.38), channel_id=1, source_target_pairs={{4,0},{8,4},{12,8},{5,1},{9,5},{13,9},{6,2},{10,6},{14,10},{7,3},{... | collective-permute-start | bytes 12488 | tf_op jit(solution)/shard_map/ppermute | solution.py:20
  122.4 5.6 %collective-permute-start.11 = (f32[1,34,130]{2,1,0:T(8,128)S(1)}, f32[1,34,130]{2,1,0:T(8,128)S(1)}, u32[]{:S(2)}, u32[]{:S(2)}) collective-permute-start(f32[1,34,130]{2,1,0:T(8,128)S(1)} %get-tuple-element.29), channel_id=1, source_target_pairs={{0,1},{1,2},{2,3},{4,5},{5,6},{6,7},{8,9},{9,10},{10,11},{12,13},{... | collective-permute-start | bytes 53048 | tf_op jit(solution)/shard_map/ppermute | solution.py:17
  126.3 5.9 %collective-permute-start.10 = (f32[1,34,130]{2,1,0:T(8,128)S(1)}, f32[1,34,130]{2,1,0:T(8,128)S(1)}, u32[]{:S(2)}, u32[]{:S(2)}) collective-permute-start(f32[1,34,130]{2,1,0:T(8,128)S(1)} %get-tuple-element.28), channel_id=1, source_target_pairs={{1,0},{2,1},{3,2},{5,4},{6,5},{7,6},{9,8},{10,9},{11,10},{13,12},{... | collective-permute-start | bytes 53048 | tf_op jit(solution)/shard_map/ppermute | solution.py:20
  190.7 3.3 collective-permute-start.12
  192.8 3.2 collective-permute-start.13
  196.1 3.2 collective-permute-start.14
  198.0 5.5 %collective-permute-start.15 = (f32[8,1,130]{2,1,0:T(1,128)S(1)}, f32[8,1,130]{2,1,0:T(1,128)S(1)}, u32[]{:S(2)}, u32[]{:S(2)}) collective-permute-start(f32[8,1,130]{2,1,0:T(1,128)S(1)} %get-tuple-element.36), channel_id=1, source_target_pairs={{4,0},{8,4},{12,8},{5,1},{9,5},{13,9},{6,2},{10,6},{14,10},{7,3},{... | collective-permute-start | bytes 12488 | tf_op jit(solution)/shard_map/ppermute | solution.py:20
  203.7 4.6 %collective-permute-start.17 = (f32[1,34,130]{2,1,0:T(8,128)S(1)}, f32[1,34,130]{2,1,0:T(8,128)S(1)}, u32[]{:S(2)}, u32[]{:S(2)}) collective-permute-start(f32[1,34,130]{2,1,0:T(8,128)S(1)} %get-tuple-element.27), channel_id=1, source_target_pairs={{0,1},{1,2},{2,3},{4,5},{5,6},{6,7},{8,9},{9,10},{10,11},{12,13},{... | collective-permute-start | bytes 53048 | tf_op jit(solution)/shard_map/ppermute | solution.py:17
  206.6 5.9 %collective-permute-start.16 = (f32[1,34,130]{2,1,0:T(8,128)S(1)}, f32[1,34,130]{2,1,0:T(8,128)S(1)}, u32[]{:S(2)}, u32[]{:S(2)}) collective-permute-start(f32[1,34,130]{2,1,0:T(8,128)S(1)} %get-tuple-element.26), channel_id=1, source_target_pairs={{1,0},{2,1},{3,2},{5,4},{6,5},{7,6},{9,8},{10,9},{11,10},{13,12},{... | collective-permute-start | bytes 53048 | tf_op jit(solution)/shard_map/ppermute | solution.py:20
  271.5 3.3 collective-permute-start.18
  273.5 3.2 collective-permute-start.19
  276.9 2.9 collective-permute-start.20
  278.4 5.5 %collective-permute-start.21 = (f32[8,1,130]{2,1,0:T(1,128)S(1)}, f32[8,1,130]{2,1,0:T(1,128)S(1)}, u32[]{:S(2)}, u32[]{:S(2)}) collective-permute-start(f32[8,1,130]{2,1,0:T(1,128)S(1)} %get-tuple-element.34), channel_id=1, source_target_pairs={{4,0},{8,4},{12,8},{5,1},{9,5},{13,9},{6,2},{10,6},{14,10},{7,3},{... | collective-permute-start | bytes 12488 | tf_op jit(solution)/shard_map/ppermute | solution.py:20
  284.1 4.7 %collective-permute-start.23 = (f32[1,34,130]{2,1,0:T(8,128)S(1)}, f32[1,34,130]{2,1,0:T(8,128)S(1)}, u32[]{:S(2)}, u32[]{:S(2)}) collective-permute-start(f32[1,34,130]{2,1,0:T(8,128)S(1)} %get-tuple-element.25), channel_id=1, source_target_pairs={{0,1},{1,2},{2,3},{4,5},{5,6},{6,7},{8,9},{9,10},{10,11},{12,13},{... | collective-permute-start | bytes 53048 | tf_op jit(solution)/shard_map/ppermute | solution.py:17
  287.1 5.9 %collective-permute-start.22 = (f32[1,34,130]{2,1,0:T(8,128)S(1)}, f32[1,34,130]{2,1,0:T(8,128)S(1)}, u32[]{:S(2)}, u32[]{:S(2)}) collective-permute-start(f32[1,34,130]{2,1,0:T(8,128)S(1)} %get-tuple-element.24), channel_id=1, source_target_pairs={{1,0},{2,1},{3,2},{5,4},{6,5},{7,6},{9,8},{10,9},{11,10},{13,12},{... | collective-permute-start | bytes 53048 | tf_op jit(solution)/shard_map/ppermute | solution.py:20
  353.0 5.2 %collective-permute-start.24 = (f32[8,32,1]{2,1,0:T(8,128)S(1)}, f32[8,32,1]{2,1,0:T(8,128)S(1)}, u32[]{:S(2)}, u32[]{:S(2)}) collective-permute-start(f32[8,32,1]{2,1,0:T(8,128)S(1)} %get-tuple-element.43), channel_id=1, source_target_pairs={{0,16},{1,17},{2,18},{3,19},{4,20},{5,21},{6,22},{7,23},{8,24},{9,... | collective-permute-start | bytes 3080 | tf_op jit(solution)/shard_map/ppermute | solution.py:17
  355.0 3.2 collective-permute-start.25
  358.4 3.4 collective-permute-start.26
  360.3 5.5 %collective-permute-start.27 = (f32[8,1,130]{2,1,0:T(1,128)S(1)}, f32[8,1,130]{2,1,0:T(1,128)S(1)}, u32[]{:S(2)}, u32[]{:S(2)}) collective-permute-start(f32[8,1,130]{2,1,0:T(1,128)S(1)} %get-tuple-element.32), channel_id=1, source_target_pairs={{4,0},{8,4},{12,8},{5,1},{9,5},{13,9},{6,2},{10,6},{14,10},{7,3},{... | collective-permute-start | bytes 12488 | tf_op jit(solution)/shard_map/ppermute | solution.py:20
  365.9 6.1 %collective-permute-start.29 = (f32[1,34,130]{2,1,0:T(8,128)S(1)}, f32[1,34,130]{2,1,0:T(8,128)S(1)}, u32[]{:S(2)}, u32[]{:S(2)}) collective-permute-start(f32[1,34,130]{2,1,0:T(8,128)S(1)} %get-tuple-element.23), channel_id=1, source_target_pairs={{0,1},{1,2},{2,3},{4,5},{5,6},{6,7},{8,9},{9,10},{10,11},{12,13},{... | collective-permute-start | bytes 53048 | tf_op jit(solution)/shard_map/ppermute | solution.py:17
  368.8 5.9 %collective-permute-start.28 = (f32[1,34,130]{2,1,0:T(8,128)S(1)}, f32[1,34,130]{2,1,0:T(8,128)S(1)}, u32[]{:S(2)}, u32[]{:S(2)}) collective-permute-start(f32[1,34,130]{2,1,0:T(8,128)S(1)} %get-tuple-element.22), channel_id=1, source_target_pairs={{1,0},{2,1},{3,2},{5,4},{6,5},{7,6},{9,8},{10,9},{11,10},{13,12},{... | collective-permute-start | bytes 53048 | tf_op jit(solution)/shard_map/ppermute | solution.py:20
  437.8 0.9 copy-start.2
where the time goes:
time: 440 us; the launch traced here: 439 us
  blocking collectives  266 us (60%)
  starting transfers between devices  54.2 us (12%)
  waiting for transfers between devices  50.1 us (11%)
  matrix products  29.2 us (7%)
  other arithmetic  17.2 us (4%)
  between operations  15.6 us (4%)
  local copies, waits for them, and re-layouts  6.18 us (1%)
    psum x11, blocking collectives, reduce_all(): return lax.psum(inner, ('slab', 'py'))  165 us
    psum x11, blocking collectives, reduce_all(): inner = lax.psum(partials, 'pz')  101 us
    ppermute x15, waiting for transfers between devices, with_halo(): lax.ppermute(lax.slice_in_dim(block, 0, width, axis=dim), axis, backward)  48.7 us
    ppermute x15, starting transfers between devices, with_halo(): lax.ppermute(lax.slice_in_dim(block, block.shape[dim] - width, None, axis...  34.5 us
    ppermute x15, starting transfers between devices, with_halo(): lax.ppermute(lax.slice_in_dim(block, 0, width, axis=dim), axis, backward)  19.7 us
    dot_general x8, matrix products, project(): jnp.einsum('kzyx,zyx->k', active, image, precision=lax.Precision.HIGHEST)  19.6 us
    dot_general x8, matrix products, remove(): jnp.einsum('k,kzyx->zyx', coeffs, active, precision=lax.Precision.HIGHEST)  9.56 us
  transfers between devices with their start and end apart: 30, of which 19 were waited for; matrix products, arithmetic and copies ran while one was open for 0% of the time, Pallas kernels for 0%

commit v1 on v0

v1 whole, which is shorter than its diff:
```python
import functools

import jax
import jax.numpy as jnp
from jax import lax
from jax.experimental import pallas as pl
from jax.experimental.pallas import tpu as pltpu
from jax.sharding import PartitionSpec as P

ITERS = 5
EPSILON = 1e-06
DIAGONAL = 6.0
FIRST_SHIFT = 8.25
MESH = pl.DeviceIdType.MESH
AXES = ("slab", "py", "pz")
UNROLLED = 64


def kernel(sizes, per_cell, x_ref, pot_ref, out_ref, tri_ref, work, ysend, zface, yface, xface,
           rz, ry, rx, slots, send_sem, recv_sem, stat_send, stat_recv):
    Z, Y, X = x_ref.shape
    S, A, B = sizes
    n = S * A * B
    slab, py, pz = (lax.axis_index(name) for name in AXES)
    me = (slab * A + py) * B + pz
    partner = lax.rem(slab + 1, S)

    def to_others(act):
        if n <= UNROLLED:
            slabs = [lax.rem(slab + i, S) for i in range(S)]
            pys = [lax.rem(py + i, A) for i in range(A)]
            pzs = [lax.rem(pz + i, B) for i in range(B)]
            far = sorted(
                ((i, j, k) for i in range(S) for j in range(A) for k in range(B)),
                key=lambda t: -(min(t[1], A - t[1]) + min(t[2], B - t[2])),
            )
            for i, j, k in far:
                if i or j or k:
                    act((slabs[i], pys[j], pzs[k]))
        else:
            def step(d, carry):
                t = lax.rem(me + d, n)
                act((t // (A * B), lax.rem(t // B, A), lax.rem(t, B)))
                return carry
            lax.fori_loop(1, n, step, 0)

    def halo_copies(p, zlo, zhi, block):
        def copy(src, dst, side, target):
            return pltpu.make_async_remote_copy(
                src_ref=src, dst_ref=dst, send_sem=send_sem.at[p, side],
                recv_sem=recv_sem.at[p, side], device_id=target, device_id_type=MESH)
        return (
            (pz < B - 1, pz > 0, copy(zhi, rz.at[p, 0], 0, (slab, py, pz + 1))),
            (pz > 0, pz < B - 1, copy(zlo, rz.at[p, 1], 1, (slab, py, pz - 1))),
            (py < A - 1, py > 0, copy(ysend.at[p, 1], ry.at[p, 0], 2, (slab, py + 1, pz))),
            (py > 0, py < A - 1, copy(ysend.at[p, 0], ry.at[p, 1], 3, (slab, py - 1, pz))),
            (None, None, copy(block, rx.at[p], 4, (partner, py, pz))),
        )

    def when(cond, act):
        if cond is None:
            act()
        else:
            pl.when(cond)(act)

    def exchange(p, zlo, zhi, block):
        copies = halo_copies(p, zlo, zhi, block)
        for sends, _, copy in copies:
            when(sends, copy.start)
        return copies

    def arrived(copies):
        for _, receives, copy in copies:
            when(receives, copy.wait_recv)

    def sent(copies):
        for sends, _, copy in copies:
            when(sends, copy.wait_send)

    def stat_copy(p, target):
        return pltpu.make_async_remote_copy(
            src_ref=slots.at[p, me], dst_ref=slots.at[p, me], send_sem=stat_send.at[p],
            recv_sem=stat_recv.at[p], device_id=target, device_id_type=MESH)

    def wait_all(p, sem):
        span = slots.at[p, pl.ds(0, n - 1)]
        pltpu.make_async_copy(span, span, sem).wait()

    lane = lax.broadcasted_iota(jnp.int32, (Y, X), 1)
    row = lax.broadcasted_iota(jnp.int32, (Y, X), 0)
    has_low = (slab > 0).astype(jnp.float32)
    has_high = (slab < S - 1).astype(jnp.float32)

    def stencil(z, own, zf, yf, xf):
        here = own(z)
        below = own(z - 1) if z > 0 else zf(0)
        above = own(z + 1) if z < Z - 1 else zf(1)
        ylow = jnp.where(row == 0, yf(0, z), pltpu.roll(here, 1, 0))
        yhigh = jnp.where(row == Y - 1, yf(1, z), pltpu.roll(here, Y - 1, 0))
        side = xf(z)
        xlow = pltpu.roll(jnp.where(lane == X - 1, side * has_low, here), 1, 1)
        xhigh = pltpu.roll(jnp.where(lane == 0, side * has_high, here), X - 1, 1)
        return (above + below) + (yhigh + ylow) + (xhigh + xlow)

    def fold(value):
        return jnp.sum(value.reshape(Y // 8, 8, X), axis=0)

    def share(p, sums):
        rows = [jnp.sum(v, axis=0, keepdims=True) for v in sums]
        height = -(-len(rows) // 8) * 8
        rows = rows + [jnp.zeros((1, X), jnp.float32)] * (height - len(rows))
        totals = jnp.sum(jnp.concatenate(rows, axis=0), axis=1, keepdims=True)
        at = lax.broadcasted_iota(jnp.int32, (height, X), 0)
        lanes = lax.broadcasted_iota(jnp.int32, (height, X), 1)
        slots[p, me] = jnp.sum(jnp.where(at == lanes, totals, 0.0), axis=0, keepdims=True)
        to_others(lambda target: stat_copy(p, target).start())

    def gathered(p, count):
        wait_all(p, stat_recv.at[p])
        total = jnp.sum(slots[p], axis=0) * per_cell
        return [jnp.broadcast_to(total[:, s:s + 1], (1, X)) for s in range(count)]

    for p in range(ITERS):
        for side, missing in ((0, pz == 0), (1, pz == B - 1)):
            @pl.when(missing)
            def _(p=p, side=side):
                rz[p, side] = jnp.zeros((Y, X), jnp.float32)
        for side, missing in ((0, py == 0), (1, py == A - 1)):
            @pl.when(missing)
            def _(p=p, side=side):
                ry[p, side] = jnp.zeros((Z, X), jnp.float32)
    for z in range(Z):
        ysend[0, 0, z:z + 1] = x_ref[z, 0:1, :]
        ysend[0, 1, z:z + 1] = x_ref[z, Y - 1:Y, :]

    barrier = pltpu.get_barrier_semaphore()
    to_others(lambda t: pl.semaphore_signal(barrier, inc=1, device_id=t, device_id_type=MESH))
    pl.semaphore_wait(barrier, n - 1)

    pending = [exchange(0, x_ref.at[0], x_ref.at[Z - 1], x_ref)]
    arrived(pending[0])

    gram = {}
    shift, lower = jnp.full((1, X), FIRST_SHIFT, jnp.float32), None
    for j in range(ITERS):
        if j == 0:
            own, zf = (lambda z: x_ref[z]), (lambda s: rz[0, s])
            yf, xf = (lambda s, z: ry[0, s, z:z + 1, :]), (lambda z: rx[0, z])
        else:
            own, zf = (lambda z: out_ref[j, z]), (lambda s: zface[j, s])
            yf, xf = (lambda s, z: yface[j, s, z:z + 1, :]), (lambda z: xface[j, z])
        for z in range(Z):
            image = ((DIAGONAL - shift) + pot_ref[z]) * own(z) - stencil(z, own, zf, yf, xf)
            if j > 0:
                image = image - lower * out_ref[j - 1, z]
            work[j, z] = image
            if j < ITERS - 1:
                ysend[j + 1, 0, z:z + 1] = image[0:1]
                ysend[j + 1, 1, z:z + 1] = image[Y - 1:Y]
        if j < ITERS - 1:
            pending.append(exchange(j + 1, work.at[j, 0], work.at[j, Z - 1], work.at[j]))
        older = [lambda z, k=k: out_ref[k, z] for k in range(j)] + [own]
        sums = [jnp.zeros((8, X), jnp.float32)] * (2 * j + 3)
        for z in range(Z):
            image, newest = work[j, z], own(z)
            for k in range(j + 1):
                v = older[k](z)
                sums[k] = sums[k] + fold(v * image)
                sums[j + 1 + k] = sums[j + 1 + k] + fold(v * newest)
            sums[2 * j + 2] = sums[2 * j + 2] + fold(image * image)
        share(j, sums)
        stats = gathered(j, 2 * j + 3)
        if j == 0:
            scale = 1.0 / jnp.sqrt(stats[1] + EPSILON)
            stats = [s * scale * scale for s in stats]
        a, square = stats[:j + 1], stats[2 * j + 2]
        for k in range(j + 1):
            gram[j, k] = gram[k, j] = stats[j + 1 + k]
        first = [a[k] + shift * gram[k, j] for k in range(j + 1)]
        if j > 0:
            first = [first[k] + lower * gram[k, j - 1] for k in range(j + 1)]
        rest = list(first)
        rest[j] = rest[j] - shift
        if j > 0:
            rest[j - 1] = rest[j - 1] - lower
        coeffs = []
        for k in range(j + 1):
            c = a[k]
            for l in range(j + 1):
                c = c - (gram[k, l] - 1.0 if k == l else gram[k, l]) * rest[l]
            coeffs.append(c)
        for k in range(j + 1):
            along = gram[k, 0] * coeffs[0]
            for l in range(1, j + 1):
                along = along + gram[k, l] * coeffs[l]
            square = square + coeffs[k] * (along - 2.0 * a[k])
        beta = jnp.sqrt(jnp.maximum(square, 0.0) + EPSILON)
        alpha = coeffs[j] + shift
        tri_ref[0:1, j:j + 1] = alpha[:, 0:1]
        tri_ref[1:2, j:j + 1] = beta[:, 0:1]
        inverse = 1.0 / beta

        if j < ITERS - 1:
            arrived(pending[j + 1])

        def follow(vectors, image):
            if j == 0:
                return (image - coeffs[0] * vectors[0]) * (inverse * scale)
            for k in range(j + 1):
                image = image - coeffs[k] * vectors[k]
            return image * inverse

        def step(get, image, put):
            vectors = [get(k) for k in range(j + 1)]
            if j == 0:
                put(0, vectors[0] * scale)
            put(j + 1, follow(vectors, image))

        def putter(ref, *index):
            def put(k, value):
                ref[(k,) + index] = value
            return put

        for z in range(Z):
            step(lambda k: x_ref[z] if j == 0 else out_ref[k, z], work[j, z], putter(out_ref, z))
            if j < ITERS - 1:
                step(lambda k: rx[0, z] if j == 0 else xface[k, z], rx[j + 1, z],
                     putter(xface, z))
        if j < ITERS - 1:
            for s in range(2):
                step(lambda k: rz[0, s] if j == 0 else zface[k, s], rz[j + 1, s],
                     putter(zface, s))
                step(lambda k: ry[0, s] if j == 0 else yface[k, s], ry[j + 1, s],
                     putter(yface, s))
        shift, lower = alpha, beta

    for copies in pending:
        sent(copies)
    for p in range(ITERS):
        wait_all(p, stat_send.at[p])


def shards(sizes, start_vector, potential):
    Z, Y, X = start_vector.shape
    n = sizes[0] * sizes[1] * sizes[2]
    f32 = jnp.float32
    vmem = pl.BlockSpec(memory_space=pltpu.VMEM)
    return tuple(pl.pallas_call(
        functools.partial(kernel, sizes, 1.0 / (start_vector.size * n)),
        out_shape=(jax.ShapeDtypeStruct((ITERS + 1, Z, Y, X), f32),
                   jax.ShapeDtypeStruct((2, ITERS), f32)),
        in_specs=[vmem, vmem],
        out_specs=(vmem, vmem),
        scratch_shapes=[
            pltpu.VMEM((ITERS, Z, Y, X), f32),
            pltpu.VMEM((ITERS, 2, Z, X), f32),
            pltpu.VMEM((ITERS, 2, Y, X), f32),
            pltpu.VMEM((ITERS, 2, Z, X), f32),
            pltpu.VMEM((ITERS, Z, Y, X), f32),
            pltpu.VMEM((ITERS, 2, Y, X), f32),
            pltpu.VMEM((ITERS, 2, Z, X), f32),
            pltpu.VMEM((ITERS, Z, Y, X), f32),
            pltpu.VMEM((ITERS, n, 1, X), f32),
            pltpu.SemaphoreType.DMA((ITERS, 5)),
            pltpu.SemaphoreType.DMA((ITERS, 5)),
            pltpu.SemaphoreType.DMA((ITERS,)),
            pltpu.SemaphoreType.DMA((ITERS,)),
        ],
        compiler_params=pltpu.CompilerParams(collective_id=0, has_side_effects=True),
    )(start_vector, potential))


def solution(mesh):
    sizes = tuple(mesh.shape[name] for name in AXES)
    in_specs = (P("pz", "py", "slab"), P("pz", "py", "slab"))
    out_specs = (P(None, "pz", "py", "slab"), P())
    return jax.shard_map(functools.partial(shards, sizes), mesh=mesh, in_specs=in_specs,
                         out_specs=out_specs, check_vma=False)
```

time: 440 us -> 38.9 us (0.09)
  blocking collectives: 266 us -> 0 us
  starting transfers between devices: 54.2 us -> 0 us
  waiting for transfers between devices: 50.1 us -> 0 us
  Pallas kernels: 0 us -> 35.5 us
  matrix products: 29.2 us -> 0 us
  other arithmetic: 17.2 us -> 0 us
  between operations: 15.6 us -> 0.65 us
    psum x22 -> x0, blocking collectives: 266 us -> none  [the longest x11 165 us: reduce_all(): return lax.psum(inner, ('slab', 'py'))]
    ppermute x30 -> x0, starting transfers between devices: 54.2 us -> none  [the longest x15 34.5 us: with_halo(): lax.ppermute(lax.slice_in_dim(block, block.shape[dim] - width, None, axis...]
    ppermute x30 -> x0, waiting for transfers between devices: 50.1 us -> none  [the longest x15 48.7 us: with_halo(): lax.ppermute(lax.slice_in_dim(block, 0, width, axis=dim), axis, backward)]
    pallas_call x0 -> x1, Pallas kernels: none -> 35.5 us  [shards(): pl.pallas_call(functools.partial(kernel, sizes, 1.0 / (start_vector.size...]
    dot_general x16 -> x0, matrix products: 29.2 us -> none  [the longest x8 19.6 us: project(): jnp.einsum('kzyx,zyx->k', active, image, precision=lax.Precision.HIGHEST)]
    reduce_sum x10 -> x0, other arithmetic: 7.39 us -> none  [the longest x5 3.27 us: shards(): jnp.sum(image * image).reshape(1)]
    slice x14 -> x0, local copies, waits for them, and re-layouts: 5.88 us -> none  [the longest x8 4.77 us: shards(): alphas.append(first_coeff[iteration] + second_coeff[iteration])]
    concatenate x10 -> x0, other arithmetic: 4.78 us -> none  [the longest x5 4.21 us: shards(): jnp.concatenate([local_second, jnp.sum(image * image).reshape(1)])]
  transfers between devices with their start and end apart: 30 -> 0, of which waited for: 19 -> 0; matrix products, arithmetic and copies ran while one was open for 0% -> 0% of each run, Pallas kernels for 0% -> 0%
where the time goes in v1:
time: 38.9 us; the launch traced here: 38.8 us
  Pallas kernels  35.5 us (91%)
  local copies, waits for them, and re-layouts  2.66 us (7%)
  between operations  0.65 us (2%)
    pallas_call x1, Pallas kernels, shards(): pl.pallas_call(functools.partial(kernel, sizes, 1.0 / (start_vector.size...  35.5 us
    unnamed x4, local copies, waits for them, and re-layouts  2.66 us

profile of v1, /device:TPU:0, one launch (start us, length us, event | category | flops | bytes accessed | tf_op | source)
XLA Modules:
  0.0 38.8 jit_solution(2226459307224856146)
XLA Ops:
  0.6 35.5 %shard_map.41 = (f32[6,8,32,128]{3,2,1,0:T(8,128)}, f32[2,5]{1,0:T(2,128)}) custom-call(f32[8,32,128]{2,1,0:T(8,128)} %x_ref.1, f32[8,32,128]{2,1,0:T(8,128)} %pot_ref.1), custom_call_target="tpu_custom_call" | custom-call | tf_op jit(solution)/shard_map/pallas_call | solution.py:248
  36.1 0.0 copy-start
  36.1 2.1 %copy.6 = f32[6,8,32,128]{3,2,1,0:T(8,128)} copy(f32[6,8,32,128]{3,2,1,0:T(8,128)} %get-tuple-element.4) | data formatting | bytes 1572864
  38.2 0.0 copy-done
  38.2 0.6 %copy.7 = f32[2,5]{1,0:T(2,128)} copy(f32[2,5]{1,0:T(2,128)S(1)} %copy-done) | data formatting | bytes 80
Async XLA Ops:
  36.1 2.1 %copy-start = (f32[2,5]{1,0:T(2,128)S(1)}, f32[2,5]{1,0:T(2,128)}, u32[]{:S(2)}) copy-start(f32[2,5]{1,0:T(2,128)} %get-tuple-element.5) | copy-start | bytes 124

commit v2 on v1

--- a/solution.py
+++ b/solution.py
@@ -10,10 +10,90 @@
 ITERS = 5
 EPSILON = 1e-06
 DIAGONAL = 6.0
-FIRST_SHIFT = 8.25
+FIRST_SHIFTS = (2.25, 8.25)
 MESH = pl.DeviceIdType.MESH
 AXES = ("slab", "py", "pz")
 UNROLLED = 64
+PLAN = (2, 3)
+
+
+def times(coeff, columns):
+    total = {}
+    for k, c in coeff.items():
+        for q, value in columns[k].items():
+            term = c * value
+            total[q] = total[q] + term if q in total else term
+    return total
+
+
+def dot(left, right):
+    total = None
+    for q, value in left.items():
+        if q in right:
+            term = value * right[q]
+            total = term if total is None else total + term
+    return 0.0 if total is None else total
+
+
+def advance(j, steps, inner, shifts, taus, removed, betas):
+    vectors = [{k: 1.0} for k in range(j + 1)]
+    image_of = [{**removed[k], k + 1: betas[k]} for k in range(j)]
+    for i in range(steps):
+        column = {j + i + 1: 1.0, j + i: shifts[i]}
+        if taus[i] is not None:
+            column[j + i - 1] = taus[i]
+        image_of.append(column)
+    gram, lowered = {}, []
+    for n in range(j, j + steps):
+        for k in range(len(lowered), n + 1):
+            lowered.append({
+                q: dot(vectors[k], {b: inner[q, b] for b in vectors[k]})
+                for q in range(n + 1)})
+            for l in range(k + 1):
+                gram[k, l] = gram[l, k] = dot(vectors[l], lowered[k])
+        known = {n: shifts[n - j]}
+        if n > j:
+            known[n - 1] = betas[n - 1]
+            rest = times(vectors[n], image_of)
+            for k, y in known.items():
+                for q, value in vectors[k].items():
+                    rest[q] = rest[q] - y * value if q in rest else -y * value
+        else:
+            if taus[0] is not None:
+                known[n - 1] = taus[0]
+            rest = {n + 1: 1.0}
+        rest_lowered = {
+            q: dot(rest, {b: inner[q, b] for b in rest}) for q in range(n + 2)}
+        along = {k: dot(vectors[k], rest_lowered) for k in range(n + 1)}
+        first = {
+            k: along[k] + dot(known, {l: gram[k, l] for l in known}) for k in range(n + 1)}
+        excess = {k: first[k] - known[k] if k in known else first[k] for k in range(n + 1)}
+        coeffs = {
+            k: along[k] - dot(excess, {
+                l: gram[k, l] - 1.0 if k == l else gram[k, l] for l in range(n + 1)})
+            for k in range(n + 1)}
+        square = dot(rest, rest_lowered)
+        for k in range(n + 1):
+            back = dot(coeffs, {l: gram[k, l] for l in range(n + 1)})
+            square = square + coeffs[k] * (back - 2.0 * along[k])
+        beta = jnp.sqrt(jnp.maximum(square, 0.0) + EPSILON)
+        inverse = 1.0 / beta
+        image = dict(rest)
+        for k in range(n + 1):
+            for q, value in vectors[k].items():
+                term = coeffs[k] * value
+                image[q] = image[q] - term if q in image else -term
+        vectors.append({q: value * inverse for q, value in image.items()})
+        removed.append({k: coeffs[k] + known[k] if k in known else coeffs[k] for k in coeffs})
+        betas.append(beta)
+    return vectors[j + 1:]
+
+
+def basis_of(j, steps, removed, betas, start):
+    if j == 0:
+        return [start + shift for shift in FIRST_SHIFTS[:steps]], [None] * steps
+    shift, beta = removed[j - 1][j - 1], betas[j - 1]
+    return [shift] * steps, [beta] + [beta * beta] * (steps - 1)
 
 
 def kernel(sizes, per_cell, x_ref, pot_ref, out_ref, tri_ref, work, ysend, zface, yface, xface,
@@ -138,83 +218,94 @@
     pl.semaphore_wait(barrier, n - 1)
 
     pending = [exchange(0, x_ref.at[0], x_ref.at[Z - 1], x_ref)]
-    arrived(pending[0])
-
-    gram = {}
-    shift, lower = jnp.full((1, X), FIRST_SHIFT, jnp.float32), None
-    for j in range(ITERS):
-        if j == 0:
-            own, zf = (lambda z: x_ref[z]), (lambda s: rz[0, s])
-            yf, xf = (lambda s, z: ry[0, s, z:z + 1, :]), (lambda z: rx[0, z])
-        else:
-            own, zf = (lambda z: out_ref[j, z]), (lambda s: zface[j, s])
-            yf, xf = (lambda s, z: yface[j, s, z:z + 1, :]), (lambda z: xface[j, z])
-        for z in range(Z):
-            image = ((DIAGONAL - shift) + pot_ref[z]) * own(z) - stencil(z, own, zf, yf, xf)
-            if j > 0:
-                image = image - lower * out_ref[j - 1, z]
-            work[j, z] = image
-            if j < ITERS - 1:
-                ysend[j + 1, 0, z:z + 1] = image[0:1]
-                ysend[j + 1, 1, z:z + 1] = image[Y - 1:Y]
-        if j < ITERS - 1:
-            pending.append(exchange(j + 1, work.at[j, 0], work.at[j, Z - 1], work.at[j]))
-        older = [lambda z, k=k: out_ref[k, z] for k in range(j)] + [own]
-        sums = [jnp.zeros((8, X), jnp.float32)] * (2 * j + 3)
-        for z in range(Z):
-            image, newest = work[j, z], own(z)
-            for k in range(j + 1):
-                v = older[k](z)
-                sums[k] = sums[k] + fold(v * image)
-                sums[j + 1 + k] = sums[j + 1 + k] + fold(v * newest)
-            sums[2 * j + 2] = sums[2 * j + 2] + fold(image * image)
-        share(j, sums)
-        stats = gathered(j, 2 * j + 3)
-        if j == 0:
-            scale = 1.0 / jnp.sqrt(stats[1] + EPSILON)
+
+    def vector(k):
+        if k == 0 and base == 0:
+            return (lambda z: x_ref[z]), *faces(0)
+        return ((lambda z: out_ref[k, z]), (lambda f: zface[k, f]),
+                (lambda f, z: yface[k, f, z:z + 1, :]), (lambda z: xface[k, z]),
+                (lambda f: yface[k, f]))
+
+    def faces(e):
+        return ((lambda f: rz[e, f]), (lambda f, z: ry[e, f, z:z + 1, :]), (lambda z: rx[e, z]),
+                (lambda f: ry[e, f]))
+
+    def powered(e):
+        return (lambda z: work[e - 1, z]), *faces(e)
+
+    removed, betas, inner, fresh = [], [], {}, range(1)
+    start = jnp.zeros((1, X), jnp.float32)
+    base, applied = 0, 0
+    for phase, steps in enumerate(PLAN):
+        last = base + steps == ITERS
+        shifts, taus = basis_of(base, steps, removed, betas, start)
+        held = [vector(k) for k in range(base + 1)]
+        pairs, sums = [], []
+
+        def measure(n, held=held, pairs=pairs, sums=sums):
+            totals = [jnp.zeros((8, X), jnp.float32)] * (n + 1)
+            for z in range(Z):
+                newest = held[n][0](z)
+                for k in range(n + 1):
+                    totals[k] = totals[k] + fold(held[k][0](z) * newest)
+            pairs.extend((k, n) for k in range(n + 1))
+            sums.extend(totals)
+
+        if phase == 0:
+            for v in fresh:
+                measure(v)
+            arrived(pending[0])
+        for i in range(steps):
+            own, zf, yf, xf, _ = held[base + i]
+            applied += 1
+            ends = applied == ITERS
+            for z in range(Z):
+                image = (((DIAGONAL - shifts[i]) + pot_ref[z]) * own(z)
+                         - stencil(z, own, zf, yf, xf))
+                if taus[i] is not None:
+                    image = image - taus[i] * held[base + i - 1][0](z)
+                work[applied - 1, z] = image
+                if not ends:
+                    ysend[applied, 0, z:z + 1] = image[0:1]
+                    ysend[applied, 1, z:z + 1] = image[Y - 1:Y]
+            held.append(powered(applied))
+            if not ends:
+                pending.append(exchange(applied, work.at[applied - 1, 0],
+                                        work.at[applied - 1, Z - 1], work.at[applied - 1]))
+            if i == 0 and phase > 0:
+                for v in fresh:
+                    measure(v)
+            measure(base + i + 1)
+            if i < steps - 1:
+                arrived(pending[applied])
+        share(phase, sums)
+        stats = gathered(phase, len(sums))
+        if phase == 0:
+            scale = 1.0 / jnp.sqrt(stats[0] + EPSILON)
             stats = [s * scale * scale for s in stats]
-        a, square = stats[:j + 1], stats[2 * j + 2]
-        for k in range(j + 1):
-            gram[j, k] = gram[k, j] = stats[j + 1 + k]
-        first = [a[k] + shift * gram[k, j] for k in range(j + 1)]
-        if j > 0:
-            first = [first[k] + lower * gram[k, j - 1] for k in range(j + 1)]
-        rest = list(first)
-        rest[j] = rest[j] - shift
-        if j > 0:
-            rest[j - 1] = rest[j - 1] - lower
-        coeffs = []
-        for k in range(j + 1):
-            c = a[k]
-            for l in range(j + 1):
-                c = c - (gram[k, l] - 1.0 if k == l else gram[k, l]) * rest[l]
-            coeffs.append(c)
-        for k in range(j + 1):
-            along = gram[k, 0] * coeffs[0]
-            for l in range(1, j + 1):
-                along = along + gram[k, l] * coeffs[l]
-            square = square + coeffs[k] * (along - 2.0 * a[k])
-        beta = jnp.sqrt(jnp.maximum(square, 0.0) + EPSILON)
-        alpha = coeffs[j] + shift
-        tri_ref[0:1, j:j + 1] = alpha[:, 0:1]
-        tri_ref[1:2, j:j + 1] = beta[:, 0:1]
-        inverse = 1.0 / beta
-
-        if j < ITERS - 1:
-            arrived(pending[j + 1])
-
-        def follow(vectors, image):
-            if j == 0:
-                return (image - coeffs[0] * vectors[0]) * (inverse * scale)
-            for k in range(j + 1):
-                image = image - coeffs[k] * vectors[k]
-            return image * inverse
-
-        def step(get, image, put):
-            vectors = [get(k) for k in range(j + 1)]
-            if j == 0:
-                put(0, vectors[0] * scale)
-            put(j + 1, follow(vectors, image))
+        for (k, l), value in zip(pairs, stats):
+            inner[k, l] = inner[l, k] = value
+        found = advance(base, steps, inner, shifts, taus, removed, betas)
+        for v in range(base, base + steps):
+            tri_ref[0:1, v:v + 1] = removed[v][v][:, 0:1]
+            tri_ref[1:2, v:v + 1] = betas[v][:, 0:1]
+        if phase == 0:
+            found = [{q: t * scale for q, t in coords.items()} for coords in found]
+        if not last:
+            arrived(pending[applied])
+
+        def fill(get, put, only_last):
+            columns = [get(held[q]) for q in range(base + steps + 1)]
+            if phase == 0 and not (only_last and len(PLAN) == 2):
+                put(0, columns[0] * scale)
+            for i, coords in enumerate(found):
+                if only_last and phase == len(PLAN) - 2 and i < steps - 1:
+                    continue
+                total = None
+                for q in sorted(coords, reverse=True):
+                    term = coords[q] * columns[q]
+                    total = term if total is None else total + term
+                put(base + 1 + i, total)
 
         def putter(ref, *index):
             def put(k, value):
@@ -222,21 +313,20 @@
             return put
 
         for z in range(Z):
-            step(lambda k: x_ref[z] if j == 0 else out_ref[k, z], work[j, z], putter(out_ref, z))
-            if j < ITERS - 1:
-                step(lambda k: rx[0, z] if j == 0 else xface[k, z], rx[j + 1, z],
-                     putter(xface, z))
-        if j < ITERS - 1:
-            for s in range(2):
-                step(lambda k: rz[0, s] if j == 0 else zface[k, s], rz[j + 1, s],
-                     putter(zface, s))
-                step(lambda k: ry[0, s] if j == 0 else yface[k, s], ry[j + 1, s],
-                     putter(yface, s))
-        shift, lower = alpha, beta
+            fill(lambda h: h[0](z), putter(out_ref, z), False)
+            if not last:
+                fill(lambda h: h[3](z), putter(xface, z), True)
+        if not last:
+            for f in range(2):
+                fill(lambda h: h[1](f), putter(zface, f), True)
+                fill(lambda h: h[4](f), putter(yface, f), True)
+        inner = {pair: value for pair, value in inner.items() if max(pair) <= base}
+        fresh = range(base + 1, base + steps + 1)
+        base += steps
 
     for copies in pending:
         sent(copies)
-    for p in range(ITERS):
+    for p in range(len(PLAN)):
         wait_all(p, stat_send.at[p])
 
 

time: 38.9 us -> 35.6 us (0.915)
  Pallas kernels: 35.5 us -> 32.1 us
    pallas_call x1, Pallas kernels: 35.5 us -> 32.1 us  [shards(): pl.pallas_call(functools.partial(kernel, sizes, 1.0 / (start_vector.size...]
where the time goes in v2:
time: 35.6 us; the launch traced here: 35.4 us
  Pallas kernels  32.1 us (90%)
  local copies, waits for them, and re-layouts  2.66 us (7%)
  between operations  0.65 us (2%)
    pallas_call x1, Pallas kernels, shards(): pl.pallas_call(functools.partial(kernel, sizes, 1.0 / (start_vector.size...  32.1 us
    unnamed x4, local copies, waits for them, and re-layouts  2.66 us

profile of v2, /device:TPU:0, one launch (start us, length us, event | category | flops | bytes accessed | tf_op | source)
XLA Modules:
  0.0 35.4 jit_solution(16515622904975968857)
XLA Ops:
  0.6 32.1 %shard_map.41 = (f32[6,8,32,128]{3,2,1,0:T(8,128)}, f32[2,5]{1,0:T(2,128)}) custom-call(f32[8,32,128]{2,1,0:T(8,128)} %x_ref.1, f32[8,32,128]{2,1,0:T(8,128)} %pot_ref.1), custom_call_target="tpu_custom_call" | custom-call | tf_op jit(solution)/shard_map/pallas_call | solution.py:338
  32.7 0.0 copy-start
  32.7 2.1 %copy.6 = f32[6,8,32,128]{3,2,1,0:T(8,128)} copy(f32[6,8,32,128]{3,2,1,0:T(8,128)} %get-tuple-element.4) | data formatting | bytes 1572864
  34.8 0.0 copy-done
  34.8 0.6 %copy.7 = f32[2,5]{1,0:T(2,128)} copy(f32[2,5]{1,0:T(2,128)S(1)} %copy-done) | data formatting | bytes 80
Async XLA Ops:
  32.7 2.1 %copy-start = (f32[2,5]{1,0:T(2,128)S(1)}, f32[2,5]{1,0:T(2,128)}, u32[]{:S(2)}) copy-start(f32[2,5]{1,0:T(2,128)} %get-tuple-element.5) | copy-start | bytes 124

commit v3 on v2

--- a/solution.py
+++ b/solution.py
@@ -10,7 +10,7 @@
 ITERS = 5
 EPSILON = 1e-06
 DIAGONAL = 6.0
-FIRST_SHIFTS = (2.25, 8.25)
+FIRST_SHIFTS = (3.5, 10.0)
 MESH = pl.DeviceIdType.MESH
 AXES = ("slab", "py", "pz")
 UNROLLED = 64

time: 35.6 us -> 35.6 us (level)
  no operation moved by 1% of the time
where the time goes in v3:
time: 35.6 us; the launch traced here: 35.4 us
  Pallas kernels  32.1 us (90%)
  local copies, waits for them, and re-layouts  2.66 us (7%)
  between operations  0.65 us (2%)
    pallas_call x1, Pallas kernels, shards(): pl.pallas_call(functools.partial(kernel, sizes, 1.0 / (start_vector.size...  32.1 us
    unnamed x4, local copies, waits for them, and re-layouts  2.66 us

profile of v3, /device:TPU:0, one launch (start us, length us, event | category | flops | bytes accessed | tf_op | source)
XLA Modules:
  0.0 35.4 jit_solution(14604928587205553165)
XLA Ops:
  0.6 32.1 %shard_map.41 = (f32[6,8,32,128]{3,2,1,0:T(8,128)}, f32[2,5]{1,0:T(2,128)}) custom-call(f32[8,32,128]{2,1,0:T(8,128)} %x_ref.1, f32[8,32,128]{2,1,0:T(8,128)} %pot_ref.1), custom_call_target="tpu_custom_call" | custom-call | tf_op jit(solution)/shard_map/pallas_call | solution.py:338
  32.7 0.0 copy-start
  32.7 2.1 %copy.6 = f32[6,8,32,128]{3,2,1,0:T(8,128)} copy(f32[6,8,32,128]{3,2,1,0:T(8,128)} %get-tuple-element.4) | data formatting | bytes 1572864
  34.8 0.0 copy-done
  34.8 0.6 %copy.7 = f32[2,5]{1,0:T(2,128)} copy(f32[2,5]{1,0:T(2,128)S(1)} %copy-done) | data formatting | bytes 80
Async XLA Ops:
  32.7 2.1 %copy-start = (f32[2,5]{1,0:T(2,128)S(1)}, f32[2,5]{1,0:T(2,128)}, u32[]{:S(2)}) copy-start(f32[2,5]{1,0:T(2,128)} %get-tuple-element.5) | copy-start | bytes 124

commit v4 on v3

--- a/solution.py
+++ b/solution.py
@@ -330,15 +330,24 @@
         wait_all(p, stat_send.at[p])
 
 
+def write_out(basis_ref, tri_ref, basis_out, tri_out, sems):
+    copies = (pltpu.make_async_copy(basis_ref, basis_out, sems.at[0]),
+              pltpu.make_async_copy(tri_ref, tri_out, sems.at[1]))
+    for copy in copies:
+        copy.start()
+    for copy in copies:
+        copy.wait()
+
+
 def shards(sizes, start_vector, potential):
     Z, Y, X = start_vector.shape
     n = sizes[0] * sizes[1] * sizes[2]
     f32 = jnp.float32
     vmem = pl.BlockSpec(memory_space=pltpu.VMEM)
-    return tuple(pl.pallas_call(
+    hbm = pl.BlockSpec(memory_space=pl.ANY)
+    basis, tri = pl.pallas_call(
         functools.partial(kernel, sizes, 1.0 / (start_vector.size * n)),
-        out_shape=(jax.ShapeDtypeStruct((ITERS + 1, Z, Y, X), f32),
-                   jax.ShapeDtypeStruct((2, ITERS), f32)),
+        out_shape=(pltpu.VMEM((ITERS + 1, Z, Y, X), f32), pltpu.VMEM((2, ITERS), f32)),
         in_specs=[vmem, vmem],
         out_specs=(vmem, vmem),
         scratch_shapes=[
@@ -357,7 +366,14 @@
             pltpu.SemaphoreType.DMA((ITERS,)),
         ],
         compiler_params=pltpu.CompilerParams(collective_id=0, has_side_effects=True),
-    )(start_vector, potential))
+    )(start_vector, potential)
+    return tuple(pl.pallas_call(
+        write_out,
+        out_shape=(jax.ShapeDtypeStruct(basis.shape, f32), jax.ShapeDtypeStruct(tri.shape, f32)),
+        in_specs=[vmem, vmem],
+        out_specs=(hbm, hbm),
+        scratch_shapes=[pltpu.SemaphoreType.DMA((2,))],
+    )(pltpu.with_memory_space_constraint(basis, pltpu.VMEM), pltpu.with_memory_space_constraint(tri, pltpu.VMEM)))
 
 
 def solution(mesh):

time: 35.6 us -> 32.9 us (0.924)
  local copies, waits for them, and re-layouts: 2.66 us -> 0 us
    unnamed x4 -> x0, local copies, waits for them, and re-layouts: 2.66 us -> none
    pallas_call x0 -> x1, Pallas kernels: none -> 0.9 us  [shards(): pl.pallas_call(write_out, out_shape=(jax.ShapeDtypeStruct(basis.shape, f3...]
    pallas_call x1, Pallas kernels: 32.1 us -> 31.2 us  [shards(): pl.pallas_call(functools.partial(kernel, sizes, 1.0 / (start_vector.size...]
where the time goes in v4:
time: 32.9 us; the launch traced here: 32.7 us
  Pallas kernels  32.1 us (98%)
  between operations  0.64 us (2%)
    pallas_call x1, Pallas kernels, shards(): pl.pallas_call(functools.partial(kernel, sizes, 1.0 / (start_vector.size...  31.2 us
    pallas_call x1, Pallas kernels, shards(): pl.pallas_call(write_out, out_shape=(jax.ShapeDtypeStruct(basis.shape, f3...  0.9 us

profile of v4, /device:TPU:0, one launch (start us, length us, event | category | flops | bytes accessed | tf_op | source)
XLA Modules:
  0.0 32.7 jit_solution(18016784945649711250)
XLA Ops:
  0.6 31.2 %shard_map.41 = (f32[6,8,32,128]{3,2,1,0:T(8,128)S(1)}, f32[2,5]{1,0:T(2,128)S(1)}) custom-call(f32[8,32,128]{2,1,0:T(8,128)} %x_ref.1, f32[8,32,128]{2,1,0:T(8,128)} %pot_ref.1), custom_call_target="tpu_custom_call" | custom-call | tf_op jit(solution)/shard_map/pallas_call | solution.py:348
  31.8 0.9 %shard_map.42 = (f32[6,8,32,128]{3,2,1,0:T(8,128)}, f32[2,5]{1,0:T(2,128)}) custom-call(f32[6,8,32,128]{3,2,1,0:T(8,128)S(1)} %get-tuple-element.4.basis_ref, f32[2,5]{1,0:T(2,128)S(1)} %get-tuple-element.5.tri_ref), custom_call_target="tpu_custom_call" | custom-call | tf_op jit(solution)/shard_map/pallas_call | solution.py:370

commit v5 on v4

--- a/solution.py
+++ b/solution.py
@@ -96,9 +96,9 @@
     return [shift] * steps, [beta] + [beta * beta] * (steps - 1)
 
 
-def kernel(sizes, per_cell, x_ref, pot_ref, out_ref, tri_ref, work, ysend, zface, yface, xface,
-           rz, ry, rx, slots, send_sem, recv_sem, stat_send, stat_recv):
-    Z, Y, X = x_ref.shape
+def kernel(sizes, per_cell, x_hbm, pot_hbm, out_ref, tri_ref, x_ref, pot_ref, work, ysend, zface, yface, xface,
+           rz, ry, rx, slots, send_sem, recv_sem, stat_send, stat_recv, load_sem):
+    Z, Y, X = x_hbm.shape
     S, A, B = sizes
     n = S * A * B
     slab, py, pz = (lax.axis_index(name) for name in AXES)
@@ -200,6 +200,12 @@
         total = jnp.sum(slots[p], axis=0) * per_cell
         return [jnp.broadcast_to(total[:, s:s + 1], (1, X)) for s in range(count)]
 
+    barrier = pltpu.get_barrier_semaphore()
+    to_others(lambda t: pl.semaphore_signal(barrier, inc=1, device_id=t, device_id_type=MESH))
+    loads = (pltpu.make_async_copy(x_hbm, x_ref, load_sem.at[0]),
+             pltpu.make_async_copy(pot_hbm, pot_ref, load_sem.at[1]))
+    for load in loads:
+        load.start()
     for p in range(ITERS):
         for side, missing in ((0, pz == 0), (1, pz == B - 1)):
             @pl.when(missing)
@@ -209,12 +215,11 @@
             @pl.when(missing)
             def _(p=p, side=side):
                 ry[p, side] = jnp.zeros((Z, X), jnp.float32)
+    for load in loads:
+        load.wait()
     for z in range(Z):
         ysend[0, 0, z:z + 1] = x_ref[z, 0:1, :]
         ysend[0, 1, z:z + 1] = x_ref[z, Y - 1:Y, :]
-
-    barrier = pltpu.get_barrier_semaphore()
-    to_others(lambda t: pl.semaphore_signal(barrier, inc=1, device_id=t, device_id_type=MESH))
     pl.semaphore_wait(barrier, n - 1)
 
     pending = [exchange(0, x_ref.at[0], x_ref.at[Z - 1], x_ref)]
@@ -348,9 +353,11 @@
     basis, tri = pl.pallas_call(
         functools.partial(kernel, sizes, 1.0 / (start_vector.size * n)),
         out_shape=(pltpu.VMEM((ITERS + 1, Z, Y, X), f32), pltpu.VMEM((2, ITERS), f32)),
-        in_specs=[vmem, vmem],
+        in_specs=[hbm, hbm],
         out_specs=(vmem, vmem),
         scratch_shapes=[
+            pltpu.VMEM((Z, Y, X), f32),
+            pltpu.VMEM((Z, Y, X), f32),
             pltpu.VMEM((ITERS, Z, Y, X), f32),
             pltpu.VMEM((ITERS, 2, Z, X), f32),
             pltpu.VMEM((ITERS, 2, Y, X), f32),
@@ -364,6 +371,7 @@
             pltpu.SemaphoreType.DMA((ITERS, 5)),
             pltpu.SemaphoreType.DMA((ITERS,)),
             pltpu.SemaphoreType.DMA((ITERS,)),
+            pltpu.SemaphoreType.DMA((2,)),
         ],
         compiler_params=pltpu.CompilerParams(collective_id=0, has_side_effects=True),
     )(start_vector, potential)

time: 32.9 us -> 31.9 us (0.970)
  Pallas kernels: 32.1 us -> 31.1 us
    pallas_call x1, Pallas kernels: 31.2 us -> 30.2 us  [shards(): pl.pallas_call(functools.partial(kernel, sizes, 1.0 / (start_vector.size...]
where the time goes in v5:
time: 31.9 us; the launch traced here: 31.8 us
  Pallas kernels  31.1 us (97%)
  between operations  0.64 us (2%)
    pallas_call x1, Pallas kernels, shards(): pl.pallas_call(functools.partial(kernel, sizes, 1.0 / (start_vector.size...  30.2 us
    pallas_call x1, Pallas kernels, shards(): pl.pallas_call(write_out, out_shape=(jax.ShapeDtypeStruct(basis.shape, f3...  0.9 us

profile of v5, /device:TPU:0, one launch (start us, length us, event | category | flops | bytes accessed | tf_op | source)
XLA Modules:
  0.0 31.8 jit_solution(11531657107276146349)
XLA Ops:
  0.6 30.2 %shard_map.41 = (f32[6,8,32,128]{3,2,1,0:T(8,128)S(1)}, f32[2,5]{1,0:T(2,128)S(1)}) custom-call(f32[8,32,128]{2,1,0:T(8,128)} %x_hbm.1, f32[8,32,128]{2,1,0:T(8,128)} %pot_hbm.1), custom_call_target="tpu_custom_call" | custom-call | tf_op jit(solution)/shard_map/pallas_call | solution.py:353
  30.9 0.9 %shard_map.42 = (f32[6,8,32,128]{3,2,1,0:T(8,128)}, f32[2,5]{1,0:T(2,128)}) custom-call(f32[6,8,32,128]{3,2,1,0:T(8,128)S(1)} %get-tuple-element.4.basis_ref, f32[2,5]{1,0:T(2,128)S(1)} %get-tuple-element.5.tri_ref), custom_call_target="tpu_custom_call" | custom-call | tf_op jit(solution)/shard_map/pallas_call | solution.py:378
